TPU v7x, 32 devices: a whole 2x2x4 slice. The times are simulated.
32 devices in a mesh: row: 2 (over x), col: 4 (over y, core), layer: 4 (over z).
Axes of the slice: x: 2, y: 2, z: 4, core: 2. Of those that a mesh axis runs over, the one named last changes fastest.
Arguments:
- a_cyclic: float32 [4, 1024, 4096], P('layer', 'row', 'col'), may hold values from -6 to 6
- a_mask: int32 [4, 8, 32], P('layer', 'row', 'col'), may hold values from 0 to 1, as said below
- b_dense: float32 [16384, 16384], P('row', ('col', 'layer')), may hold values from -0.21875 to 0.21875
- b_mask: int32 [128, 128], P('row', ('col', 'layer')), may hold values from 0 to 1, as said below
Outputs:
- product: float32 [1024, 16384], P('row', ('col', 'layer'))
Inputs may be any that keep to these rules, and one draw needn't show every extreme that they name: For each l, each run of 4 block rows starting at a multiple of 4 and each run of 8 block columns starting at a multiple of 8, those blocks of a_mask[l] hold 1 to 12 ones. In every draw, for some l and some row run, the groups of all 4 column runs hold exactly 12. `b_mask`: take the block rows r * 64 to (r + 1) * 64 - 1, a residue d modulo 4, and the block columns g * 8 to (g + 1) * 8 - 1: the blocks among them whose row index is d modulo 4 hold 1 to 48 ones. In every draw, for some r, d and c, the groups of all g from c * 4 to c * 4 + 3 hold exactly 48.
All inputs are finite; a program needn't handle non-finite values.
Results may differ from a plain program's by a relative error of at most 0.00007.
Values sent between devices are 32-bit elements; how exact they have to be, the bound alone decides.
No kernel may reach another device: no remote copies, remote signals or barrier semaphores. Data moves between devices by JAX's collectives and lax.ppermute only.
A program may use at most 256 MiB of HBM per device.

v0:
```python
import jax
import jax.numpy as jnp
from jax import lax
from jax.sharding import PartitionSpec as P

precise = lax.Precision.HIGHEST


def to_blocks(matrix, block_size):
    row_blocks = matrix.shape[0] // block_size
    col_blocks = matrix.shape[1] // block_size
    shaped = matrix.reshape(row_blocks, block_size, col_blocks, block_size).transpose(0, 2, 1, 3)
    return shaped.reshape(row_blocks * col_blocks, block_size, block_size)


def pack_blocks(blocks, is_live, capacity):
    total_places = is_live.shape[0]
    rank_of = jnp.cumsum(is_live) - 1
    slot_numbers = jnp.arange(capacity, dtype=jnp.int32)
    chosen = (is_live[None, :] > 0) & (rank_of[None, :] == slot_numbers[:, None])
    weights = chosen.astype(jnp.float32)
    packed = jnp.einsum("cg,gxy->cxy", weights, blocks, precision=precise)
    places = jnp.arange(total_places, dtype=jnp.int32)
    any_match = jnp.any(chosen, axis=1)
    position = jnp.sum(jnp.where(chosen, places[None, :], 0), axis=1)
    slot_ids = jnp.where(any_match, position, -1)
    return (packed, slot_ids)


def lookup_table(gathered, key_of, key_count):
    slot_count = gathered.shape[0]
    key_values = jnp.arange(key_count, dtype=jnp.int32)
    matches = key_of[:, None] == key_values[None, :]
    any_match = jnp.any(matches, axis=0)
    slot_numbers = jnp.arange(slot_count, dtype=jnp.int32)
    slot_index = jnp.sum(jnp.where(matches, slot_numbers[:, None], 0), axis=0)
    slot_of = jnp.where(any_match, slot_index, slot_count)
    padded = jnp.concatenate([gathered, jnp.zeros((1,) + gathered.shape[1:], jnp.float32)], axis=0)
    return (padded, slot_of)


def accumulate(running, slot_data, slot_ids, source, padded, slot_of, k_step, jwidth):
    row_blocks = running.shape[0]
    is_live = slot_ids >= 0
    clipped = jnp.maximum(slot_ids, 0)
    k_index = source * k_step + clipped // jwidth
    column = clipped % jwidth
    rows_here = jnp.arange(row_blocks, dtype=jnp.int32)
    where_rows = slot_of[k_index[:, None] * row_blocks + rows_here[None, :]]
    a_pieces = padded[where_rows]
    b_pieces = jnp.where(is_live[:, None, None], slot_data, 0.0)
    products = jnp.einsum("smxa,sab->smxb", a_pieces, b_pieces, precision=precise)
    spread = (
        (column[:, None] == jnp.arange(jwidth, dtype=jnp.int32)[None, :]) & is_live[:, None]
    ).astype(jnp.float32)
    return running + jnp.einsum("smxb,sj->mxjb", products, spread, precision=precise)


def make_folder(padded, slot_of, k_step, jwidth, shard):

    def fold_piece(running, portion, offset):
        slot_data, slot_ids = portion
        sources = slot_data.shape[0] // shard
        slot_groups = slot_data.reshape((sources, shard) + slot_data.shape[1:])
        id_groups = slot_ids.reshape(sources, shard)
        source_rows = jnp.arange(sources, dtype=jnp.int32)

        def add_source(carry, inputs):
            group_slots, group_ids, source = inputs
            return (
                accumulate(carry, group_slots, group_ids, source, padded, slot_of, k_step, jwidth),
                None,
            )

        result, unused = lax.scan(add_source, running, (slot_groups, id_groups, source_rows))
        return result

    return fold_piece


def on_device(a_cyclic, a_mask, b_dense, b_mask):
    block_size = a_cyclic.shape[1] // a_mask.shape[1]
    layer_count = lax.axis_size("layer")
    row_count = lax.axis_size("row")
    row_blocks = a_mask.shape[1]
    q_blocks = a_mask.shape[2]
    k_run = b_mask.shape[0]
    j_run = b_mask.shape[1]
    per_layer = k_run // layer_count
    a_capacity = max(2, row_blocks * q_blocks * 3 // 8)
    b_capacity = max(2, per_layer * j_run * 3 // 8)
    a_blocks = to_blocks(a_cyclic[0], block_size)
    a_slots, a_ids = pack_blocks(a_blocks, a_mask[0].reshape(-1), a_capacity)
    b_blocks = to_blocks(b_dense, block_size)
    gathered, gathered_ids = (
        lax.all_gather(a_slots, ("col", "layer"), axis=0, tiled=True),
        lax.all_gather(a_ids, ("col", "layer"), axis=0, tiled=True),
    )
    from_device = jnp.arange(gathered.shape[0], dtype=jnp.int32) // a_capacity
    from_col = from_device // layer_count
    from_layer = from_device % layer_count
    clipped = jnp.maximum(gathered_ids, 0)
    k_index = (from_col * q_blocks + clipped % q_blocks) * layer_count + from_layer
    key_of = jnp.where(gathered_ids >= 0, k_index * row_blocks + clipped // q_blocks, -1)
    padded, slot_of = lookup_table(gathered, key_of, k_run * row_count * row_blocks)
    b_slots, b_ids = pack_blocks(b_blocks, b_mask.reshape(-1), layer_count * b_capacity)
    zero_sum = jnp.zeros((row_blocks, block_size, j_run, block_size), jnp.float32)
    folder = make_folder(padded, slot_of, k_run, j_run, layer_count * b_capacity)
    running = folder(
        zero_sum,
        (
            lax.all_gather(b_slots, "row", axis=0, tiled=True),
            lax.all_gather(b_ids, "row", axis=0, tiled=True),
        ),
        jnp.int32(0),
    )
    return running.reshape(row_blocks * block_size, j_run * block_size)


def solution(mesh):
    placed = (
        P("layer", "row", "col"),
        P("layer", "row", "col"),
        P("row", ("col", "layer")),
        P("row", ("col", "layer")),
    )
    return jax.shard_map(
        on_device, mesh=mesh, in_specs=placed, out_specs=P("row", ("col", "layer")), check_vma=False
    )
```

profile of v0, /device:TPU:0, one launch (start us, length us, event | category | flops | bytes accessed | tf_op | source)
XLA Modules:
  0.0 718.8 jit_solution(1314038571946012761)
XLA Ops:
  6.5 0.8 reshape.258
  7.3 0.7 broadcast_compare_fusion.2
  8.0 0.1 add_reduce_fusion
  8.2 2.1 copy.28
  10.3 0.8 fusion.21
  11.2 1.1 copy.22
  12.4 0.8 copy.19
  13.2 0.3 reduce-window.19
  13.6 0.7 broadcast_compare_fusion.1
  14.3 0.1 copy.18
  14.5 27.6 %copy.29 = f32[1024,8,8,128]{3,2,1,0:T(8,128)} copy(f32[1024,8,8,128]{3,1,2,0:T(8,128)} %bitcast.104) | data formatting | bytes 67108864
  42.2 0.1 slice_reduce_fusion
  42.4 25.7 %fusion.18 = f32[192,128,128]{2,0,1:T(8,128)} fusion(s32[512]{0:T(512)S(1)} %add_bitcast_fusion, pred[512]{0:T(512)(128)(4,1)S(1)} %gt.30, f32[64,128,8,128]{3,2,1,0:T(8,128)} %bitcast.101), kind=kOutput, calls=%fused_computation.34 | convolution fusion | flops 19327549440 | bytes 46139904 | tf_op jit(solution)/shard_map/cg,gxy->cxy/dot_general | solution.py:22
  68.1 0.6 copy-done.1
  68.7 0.6 dynamic-slice.1
  69.3 0.6 dynamic-slice
  70.5 0.1 fusion.27
  70.6 0.2 select_reduce_fusion.1
  70.8 0.1 select_dynamic-update-slice_fusion
  70.9 4.7 all-reduce.1
  76.3 0.1 fusion.33
  76.4 0.1 select_reduce_fusion.2
  76.6 12.7 %all-reduce.2 = s32[192]{0:T(256)S(1)} all-reduce(s32[192]{0:T(256)S(1)} %select_dynamic-update-slice_fusion.1), channel_id=1, replica_groups=mesh['row'=2,'col'=4,'layer'=4] {'col','layer'}, use_global_device_ids=true, to_apply=%add.2 | all-reduce | flops 192 | bytes 1536
  89.4 0.1 fusion.24
  89.5 0.1 select_reduce_fusion
  89.7 26.1 %all-gather.3.cloned.1.call-done = f32[192,128,128]{2,1,0:T(8,128)} async-done(((f32[12,128,128]{2,1,0:T(8,128)}), f32[192,128,128]{2,1,0:T(8,128)}) %all-gather.3.cloned.1.call-update) | async-done | bytes 12582928 | tf_op jit(solution)/shard_map/all_gather | solution.py:96
  115.7 15.9 %concatenate.3 = f32[193,128,128]{2,1,0:T(8,128)} pad(f32[192,128,128]{2,1,0:T(8,128)} %all-gather.3.cloned.1.call-done, f32[]{:T(128)} %constant.149.clone.1), padding=0_1x0_0x0_0 | pad | bytes 25231364 | tf_op jit(solution)/shard_map/concatenate | solution.py:38
  131.6 279.9 %all-gather.5.cloned.1.call-done = f32[384,128,128]{2,0,1:T(8,128)} async-done(((f32[192,128,128]{2,0,1:T(8,128)}), f32[384,128,128]{2,0,1:T(8,128)}) %all-gather.5.cloned.1.call-update) | async-done | bytes 25165840 | tf_op jit(solution)/shard_map/all_gather | solution.py:112
  411.5 298.6 %while.13 = (s32[]{:T(128)}, f32[4,128,8,128]{3,2,1,0:T(8,128)S(1)}, s32[2,192]{1,0:T(2,128)S(1)}, s32[2]{0:T(128)S(1)}, s32[512]{0:T(512)S(1)}, /*index=5*/f32[...) while((s32[]{:T(128)}, ...), condition=%wide.region_10.11_spmd.clone, body=%wide.region_9.10_spmd.clone.sunk | while | flops 20539518976 | bytes 293664320 | solution.py:75
  411.6 0.6 dynamic_slice.43
  412.9 0.1 reshape.273
  413.1 5.0 gather_fusion
  418.1 0.1 gather.26
  418.2 0.1 reshape.274
  418.3 26.5 %gather_fusion.1 = f32[768,128,128]{2,1,0:T(8,128)} fusion(f32[193,128,128]{2,1,0:T(8,128)} %get-tuple-element.243, s32[1024]{0:T(1024)S(1)} %pad_clamp_fusion.5), kind=kCustom, calls=%fused_computation.1.clone.clone.1 | custom fusion | bytes 100666368 | tf_op jit(solution)/shard_map/while/body/eval_jaxpr/gather | solution.py:50
  444.8 10.7 %constant_dynamic-slice_fusion.3 = f32[1,192,128,128]{3,1,0,2:T(8,128)} fusion(f32[2,192,128,128]{3,1,0,2:T(8,128)} %get-tuple-element.244, s32[]{:T(128)} %get-tuple-element.228), kind=kLoop, calls=%fused_computation.30.clone.1 | loop fusion | bytes 25165828 | tf_op jit(solution)/shard_map/while/body/jit(dynamic_index_in_dim)/dynamic_slice | solution.py:75
  455.5 52.8 %fusion.53 = f32[192,4,128,128]{3,2,1,0:T(8,128)} fusion(f32[192,4,128,128]{3,2,1,0:T(8,128)} %bitcast.100, f32[1,192,128,128]{3,1,0,2:T(8,128)} %constant_dynamic-slice_fusion.3, pred[192]{0:T(512)(128)(4,1)S(1)} %get-tuple-element.216), kind=kOutput, calls=%fused_computation.7.clone.2 | convolution fusion | flops 19330498560 | bytes 113246400 | tf_op jit(solution)/shard_map/while/body/eval_jaxpr/smxa,sab->smxb/dot_general | solution.py:52
  508.4 52.5 %bitcast_add_fusion.2 = f32[4,128,8,128]{3,2,1,0:T(8,128)S(1)} fusion(f32[4,128,8,128]{3,2,1,0:T(8,128)S(1)} %get-tuple-element.229, f32[192,4,128,128]{3,2,1,0:T(8,128)} %fusion.53, pred[]{:T(512)S(6)} %compare.15, s32[192]{0:T(256)S(1)} %get-tuple-element.217, pred[192]{0:T(512)(128)(4,1)S(1)} %get-tuple-element.216), kind=kOutput, calls=%fused_computation.10.clone.1 | convolution fusion | flops 1209011200 | bytes 54526912 | tf_op jit(solution)/shard_map/while/body/eval_jaxpr/smxb,sj->mxjb/dot_general | solution.py:56
  561.0 0.6 dynamic_slice.43
  562.3 0.1 reshape.273
  562.5 5.0 gather_fusion
  567.5 0.1 gather.26
  567.6 0.1 reshape.274
  567.7 26.3 %gather_fusion.1 = f32[768,128,128]{2,1,0:T(8,128)} fusion(f32[193,128,128]{2,1,0:T(8,128)} %get-tuple-element.243, s32[1024]{0:T(1024)S(1)} %pad_clamp_fusion.5), kind=kCustom, calls=%fused_computation.1.clone.clone.1 | custom fusion | bytes 100666368 | tf_op jit(solution)/shard_map/while/body/eval_jaxpr/gather | solution.py:50
  594.1 10.7 %constant_dynamic-slice_fusion.3 = f32[1,192,128,128]{3,1,0,2:T(8,128)} fusion(f32[2,192,128,128]{3,1,0,2:T(8,128)} %get-tuple-element.244, s32[]{:T(128)} %get-tuple-element.228), kind=kLoop, calls=%fused_computation.30.clone.1 | loop fusion | bytes 25165828 | tf_op jit(solution)/shard_map/while/body/jit(dynamic_index_in_dim)/dynamic_slice | solution.py:75
  604.8 52.8 %fusion.53 = f32[192,4,128,128]{3,2,1,0:T(8,128)} fusion(f32[192,4,128,128]{3,2,1,0:T(8,128)} %bitcast.100, f32[1,192,128,128]{3,1,0,2:T(8,128)} %constant_dynamic-slice_fusion.3, pred[192]{0:T(512)(128)(4,1)S(1)} %get-tuple-element.216), kind=kOutput, calls=%fused_computation.7.clone.2 | convolution fusion | flops 19330498560 | bytes 113246400 | tf_op jit(solution)/shard_map/while/body/eval_jaxpr/smxa,sab->smxb/dot_general | solution.py:52
  657.6 52.5 %bitcast_add_fusion.2 = f32[4,128,8,128]{3,2,1,0:T(8,128)S(1)} fusion(f32[4,128,8,128]{3,2,1,0:T(8,128)S(1)} %get-tuple-element.229, f32[192,4,128,128]{3,2,1,0:T(8,128)} %fusion.53, pred[]{:T(512)S(6)} %compare.15, s32[192]{0:T(256)S(1)} %get-tuple-element.217, pred[192]{0:T(512)(128)(4,1)S(1)} %get-tuple-element.216), kind=kOutput, calls=%fused_computation.10.clone.1 | convolution fusion | flops 1209011200 | bytes 54526912 | tf_op jit(solution)/shard_map/while/body/eval_jaxpr/smxb,sj->mxjb/dot_general | solution.py:56
  710.2 1.8 copy.52
  (36 shorter events, 1.2 us)
Async XLA Ops:
  6.5 109.2 %all-gather.3.cloned.1.call-start = ((), (), s32[]{:S(2)}) async-start(), calls=%async_computation | async-start | bytes 13369344 | tf_op jit(solution)/shard_map/all_gather | solution.py:96
  12.3 399.2 %all-gather.5.cloned.1.call-start = ((), (), s32[]{:S(2)}) async-start(), calls=%async_computation.1 | async-start | bytes 37748736 | tf_op jit(solution)/shard_map/all_gather | solution.py:112
  68.0 0.7 copy-start.1
  68.0 1.3 copy-start
Sparse Core Ops, SparseCore 0:
  12.4 103.2 all-gather.2
  117.3 294.2 all-gather.4
where the time goes:
time: 720 us; the launch traced here: 719 us
  waiting for transfers between devices  306 us (42%)
  matrix products  237 us (33%)
  local copies, waits for them, and re-layouts  139 us (19%)
  blocking collectives  17.4 us (2%)
  between operations  14.7 us (2%)
    all_gather x1, waiting for transfers between devices, on_device(): lax.all_gather(b_slots, 'row', axis=0, tiled=True)  280 us
    dot_general x2, matrix products, accumulate(): jnp.einsum('smxa,sab->smxb', a_pieces, b_pieces, precision=precise)  106 us
    dot_general x2, matrix products, accumulate(): jnp.einsum('smxb,sj->mxjb', products, spread, precision=precise)  105 us
    gather x2, local copies, waits for them, and re-layouts, accumulate(): a_pieces = padded[where_rows]  52.8 us
    unnamed x12, local copies, waits for them, and re-layouts  34.1 us
    dot_general x2, matrix products, pack_blocks(): packed = jnp.einsum('cg,gxy->cxy', weights, blocks, precision=precise)  26.5 us
    all_gather x1, waiting for transfers between devices, on_device(): lax.all_gather(a_slots, ('col', 'layer'), axis=0, tiled=True)  26.1 us
    dynamic_slice x4, local copies, waits for them, and re-layouts, fold_piece(): lax.scan(add_source, running, (slot_groups, id_groups, source_rows))  22.6 us
  transfers between devices with their start and end apart: 2, of which 2 were waited for; matrix products, arithmetic and copies ran while one was open for 10% of the time, Pallas kernels for 0%

commit v1 on v0

v1 whole, which is shorter than its diff:
```python
import jax
import jax.numpy as jnp
from jax import lax
from jax.experimental import pallas as pl
from jax.experimental.pallas import tpu as pltpu
from jax.sharding import PartitionSpec as P

META = 8
GROUP = 4
CHUNK = 8
PARTS = 2
SPLIT = 4
AXES = ("row", "col", "layer")
SMEM = pl.BlockSpec(memory_space=pltpu.SMEM)
VMEM = pl.BlockSpec(memory_space=pltpu.VMEM)
ANY = pl.BlockSpec(memory_space=pl.ANY)
HBM = pl.BlockSpec(memory_space=pltpu.HBM)


def split_wide(x):
    hi = x.astype(jnp.bfloat16)
    lo = (x - hi.astype(jnp.float32)).astype(jnp.bfloat16)
    return jnp.concatenate([hi, lo], axis=1)


def pack_units(base, a_local, a_mask, slots, n_layer, bs):
    row_blocks, q_blocks = a_mask.shape
    rows = slots * bs + META

    def body(base_ref, mask_ref, a_ref, out_ref, sem):
        lane = lax.broadcasted_iota(jnp.int32, (META, bs), 1)

        def visit(i, carry):
            n, codes = carry
            for q in range(q_blocks):
                live = mask_ref[i, q] > 0
                code = ((base_ref[0] * q_blocks + q) * n_layer + base_ref[1]) * row_blocks + i

                @pl.when(live)
                def _(n=n, q=q):
                    part = jnp.int32(0)
                    for p in range(1, PARTS):
                        part = part + (n >= p * slots).astype(jnp.int32)
                    pltpu.make_async_copy(
                        a_ref.at[pl.ds(pl.multiple_of(i * bs, bs), bs), pl.ds(q * bs, bs)],
                        out_ref.at[part, pl.ds(pl.multiple_of((n - part * slots) * bs, bs), bs), :],
                        sem,
                    ).start()

                value = jnp.where(live, code, -1).astype(jnp.float32)
                codes = tuple(jnp.where(lane == n - p * slots, value, codes[p]) for p in range(PARTS))
                n = n + live.astype(jnp.int32)
            return n, codes

        empty = jnp.full((META, bs), -1.0, jnp.float32)
        count, codes = lax.fori_loop(0, row_blocks, visit, (jnp.int32(0), (empty,) * PARTS))
        for p in range(PARTS):
            out_ref[p, pl.ds(slots * bs, META), :] = codes[p]

        def drain(n, carry):
            pltpu.make_async_copy(
                a_ref.at[pl.ds(0, bs), pl.ds(0, bs)], out_ref.at[0, pl.ds(0, bs), :], sem
            ).wait()
            return carry

        lax.fori_loop(0, count, drain, 0)

    return pl.pallas_call(
        body,
        out_shape=jax.ShapeDtypeStruct((PARTS, rows, bs), jnp.float32),
        in_specs=[SMEM, SMEM, ANY],
        out_specs=VMEM,
        scratch_shapes=[pltpu.SemaphoreType.DMA],
        name="pack_units",
    )(base, a_mask, a_local)


def pack_b(b_mask, b_dense, b_cap, bs):
    k_run, j_run = b_mask.shape
    slots = (-(-b_cap // CHUNK) + j_run) * CHUNK

    def body(bm_ref, b_ref, out_ref, k_ref, start_ref, count_ref, b_f32, b_wide, sem, out_sem):
        def column(j, carry):
            n, live_blocks = carry
            start_ref[j] = n
            col = pl.multiple_of(j * bs, bs)

            def visit(t, n):
                for e in range(4):
                    k = t * 4 + e
                    live = bm_ref[k, j] > 0

                    @pl.when(live)
                    def _(k=k, n=n):
                        k_ref[n] = k
                        pltpu.make_async_copy(
                            b_ref.at[pl.ds(pl.multiple_of(k * bs, bs), bs), pl.ds(col, bs)], b_f32.at[n], sem
                        ).start()

                    n = n + live.astype(jnp.int32)
                return n

            m = lax.fori_loop(0, k_run // 4, visit, n)
            count_ref[j] = m
            return (m + CHUNK - 1) // CHUNK * CHUNK, live_blocks + m - n

        n, blocks = lax.fori_loop(0, j_run, column, (jnp.int32(0), jnp.int32(0)))
        start_ref[j_run] = n
        chunks = n // CHUNK
        b_wide[slots] = jnp.zeros((bs, 2 * bs), jnp.bfloat16)
        zero = pltpu.make_async_copy(b_wide.at[pl.ds(slots, 1)], out_ref.at[pl.ds(slots, 1)], out_sem.at[0])
        zero.start()

        def arrive(t, carry):
            pltpu.make_async_copy(b_ref.at[pl.ds(0, bs), pl.ds(0, bs)], b_f32.at[0], sem).wait()
            return carry

        lax.fori_loop(0, blocks, arrive, 0)

        def widen(t, carry):
            for e in range(CHUNK):
                b_wide[t * CHUNK + e] = split_wide(b_f32[t * CHUNK + e])
            pltpu.make_async_copy(
                b_wide.at[pl.ds(t * CHUNK, CHUNK)], out_ref.at[pl.ds(t * CHUNK, CHUNK)], out_sem.at[1]
            ).start()
            return carry

        lax.fori_loop(0, chunks, widen, 0)

        def leave(t, carry):
            pltpu.make_async_copy(
                b_wide.at[pl.ds(0, CHUNK)], out_ref.at[pl.ds(0, CHUNK)], out_sem.at[1]
            ).wait()
            return carry

        lax.fori_loop(0, chunks, leave, 0)
        zero.wait()

    return pl.pallas_call(
        body,
        out_shape=(
            jax.ShapeDtypeStruct((slots + 1, bs, 2 * bs), jnp.bfloat16),
            jax.ShapeDtypeStruct((slots,), jnp.int32),
            jax.ShapeDtypeStruct((j_run + 1,), jnp.int32),
            jax.ShapeDtypeStruct((j_run,), jnp.int32),
        ),
        in_specs=[SMEM, ANY],
        out_specs=(ANY, SMEM, SMEM, SMEM),
        scratch_shapes=[
            pltpu.VMEM((slots, bs, bs), jnp.float32),
            pltpu.VMEM((slots + 1, bs, 2 * bs), jnp.bfloat16),
            pltpu.SemaphoreType.DMA,
            pltpu.SemaphoreType.DMA((2,)),
        ],
        name="pack_b",
        compiler_params=pltpu.CompilerParams(vmem_limit_bytes=60 * 1024 * 1024),
    )(b_mask, b_dense)


def multiply_run(units, packed, k_run, row_blocks, slots, bs, columns=None, k_base=None):
    b_wide, b_k, b_start, b_end = packed
    b_slots = b_wide.shape[0] - 1
    j_from, j_to = columns or (0, b_end.shape[0])
    j_run = j_to - j_from
    arrays = list(dict.fromkeys(id(x) for x, _ in units))
    held = {id(x): x for x, _ in units}
    places = [(arrays.index(id(x)), at) for x, at in units]
    n_src = len(units)
    pad = k_run + GROUP
    split = SPLIT if row_blocks % SPLIT == 0 else 1
    part = row_blocks * bs // split
    per_part = row_blocks // split
    height = row_blocks * bs
    row_bits = row_blocks.bit_length() - 1 if row_blocks & (row_blocks - 1) == 0 else None

    def body(bk_ref, bs_ref, be_ref, base_ref, bw_ref, *rest):
        u_refs = [rest[ref].at[at] for ref, at in places]
        (out_ref, a_f32, a_wide, b_all, acc, codes, any_a, klist, blist,
         c_sem, a_sem, b_sem, z_sem) = rest[len(arrays):]
        for u in range(n_src):
            pltpu.make_async_copy(u_refs[u].at[pl.ds(slots * bs, META), :], codes.at[u], c_sem).start()
        for u in range(n_src):
            pltpu.make_async_copy(u_refs[u].at[pl.ds(0, slots * bs), :], a_f32.at[u], a_sem.at[u]).start()

        def b_copy(t, j):
            return pltpu.make_async_copy(
                bw_ref.at[pl.ds(t * CHUNK, CHUNK)], b_all.at[pl.ds(t * CHUNK, CHUNK)], b_sem.at[j]
            )

        for j in range(j_run):
            def b_load(t, carry, j=j):
                b_copy(t, j).start()
                return carry

            lax.fori_loop(bs_ref[j_from + j] // CHUNK, bs_ref[j_from + j + 1] // CHUNK, b_load, 0)
        zero = pltpu.make_async_copy(bw_ref.at[pl.ds(b_slots, 1)], b_all.at[pl.ds(b_slots, 1)], z_sem)
        zero.start()

        def wipe(k, carry):
            for r in range(split):
                any_a[k * split + r] = 0
            a_wide[k] = jnp.zeros((height, 2 * bs), jnp.bfloat16)
            return carry

        lax.fori_loop(0, k_run, wipe, 0)
        for u in range(n_src):
            pltpu.make_async_copy(u_refs[u].at[pl.ds(slots * bs, META), :], codes.at[u], c_sem).wait()
        base = base_ref[0] * (k_run * row_blocks)
        for u in range(n_src):
            pltpu.make_async_copy(
                u_refs[u].at[pl.ds(0, slots * bs), :], a_f32.at[u], a_sem.at[u]
            ).wait()

            for s in range(slots):
                code = codes[u, 0, s].astype(jnp.int32) - base
                live = jnp.logical_and(code >= 0, code < k_run * row_blocks)
                code = jnp.where(live, code, k_run * row_blocks)
                k = lax.shift_right_logical(code, row_bits) if row_bits is not None else code // row_blocks
                row = pl.multiple_of((code - k * row_blocks) * bs, bs)
                any_a[code // per_part] = 1
                a_wide[k, pl.ds(row, bs), :] = split_wide(a_f32[u, s * bs:(s + 1) * bs, :])

        zero.wait()

        for j in range(j_run):
            def choose(t, taken):
                k = bk_ref[t]
                out = []
                for r in range(split):
                    klist[r, taken[r]] = k
                    blist[r, taken[r]] = t
                    out.append(taken[r] + any_a[k * split + r])
                return tuple(out)

            taken = lax.fori_loop(
                bs_ref[j_from + j], be_ref[j_from + j], choose, (jnp.int32(0),) * split
            )
            longest = taken[0]
            for r in range(1, split):
                longest = jnp.maximum(longest, taken[r])
            groups = (longest + GROUP - 1) // GROUP
            for r in range(split):
                def blank(n, carry, r=r):
                    klist[r, n] = 0
                    blist[r, n] = b_slots
                    return carry

                lax.fori_loop(taken[r], groups * GROUP, blank, 0)

            def b_arrive(t, carry, j=j):
                b_copy(t, j).wait()
                return carry

            lax.fori_loop(bs_ref[j_from + j] // CHUNK, bs_ref[j_from + j + 1] // CHUNK, b_arrive, 0)
            acc[...] = jnp.zeros(acc.shape, jnp.float32)

            def step(t, carry):
                for r in range(split):
                    rows = slice(r * part, (r + 1) * part)
                    left = []
                    right = []
                    for e in range(GROUP):
                        left.append(a_wide[klist[r, t * GROUP + e], rows, :])
                        w = b_all[blist[r, t * GROUP + e]]
                        right.extend([w, w])
                    acc[rows, :] += jnp.dot(
                        jnp.concatenate(left, axis=1),
                        jnp.concatenate(right, axis=0),
                        preferred_element_type=jnp.float32,
                    )
                return carry

            lax.fori_loop(0, groups, step, 0)
            out_ref[:, j * bs:(j + 1) * bs] = acc[:, :bs] + acc[:, bs:]

    limit = (n_src * slots * bs * bs * 4 + (k_run + 1) * height * 4 * bs + (b_slots + 1) * bs * bs * 4
             + height * 2 * bs * 4 + height * j_run * bs * 4) * 17 // 16 + (2 << 20)
    if k_base is None:
        k_base = jnp.zeros((1,), jnp.int32)
    return pl.pallas_call(
        body,
        out_shape=jax.ShapeDtypeStruct((height, j_run * bs), jnp.float32),
        in_specs=[SMEM, SMEM, SMEM, SMEM, HBM] + [ANY] * len(arrays),
        out_specs=VMEM,
        scratch_shapes=[
            pltpu.VMEM((n_src, slots * bs, bs), jnp.float32),
            pltpu.VMEM((k_run + 1, height, 2 * bs), jnp.bfloat16),
            pltpu.VMEM((b_slots + 1, bs, 2 * bs), jnp.bfloat16),
            pltpu.VMEM((height, 2 * bs), jnp.float32),
            pltpu.SMEM((n_src, META, bs), jnp.float32),
            pltpu.SMEM(((k_run + 1) * split,), jnp.int32),
            pltpu.SMEM((split, pad), jnp.int32),
            pltpu.SMEM((split, pad), jnp.int32),
            pltpu.SemaphoreType.DMA,
            pltpu.SemaphoreType.DMA((n_src,)),
            pltpu.SemaphoreType.DMA((j_run,)),
            pltpu.SemaphoreType.DMA,
        ],
        name="multiply_run",
        compiler_params=pltpu.CompilerParams(vmem_limit_bytes=limit),
    )(b_k, b_start, b_end, k_base, b_wide, *[held[key] for key in arrays])


def on_device(a_cyclic, a_mask, b_dense, b_mask):
    bs = a_cyclic.shape[1] // a_mask.shape[1]
    n_row, n_col, n_layer = (lax.axis_size(name) for name in AXES)
    row_blocks, q_blocks = a_mask.shape[1:]
    k_run, j_run = b_mask.shape
    cap = max(2, row_blocks * q_blocks * 3 // 8)
    slots = -(-cap // PARTS)
    b_cap = n_layer * max(2, k_run // n_layer * j_run * 3 // 8)
    row, col, layer = (lax.axis_index(name) for name in AXES)
    paired = n_row == 2 and n_col % 2 == 0
    wide = n_col // 2 if paired else n_col
    base = jnp.stack([col % wide, layer]).astype(jnp.int32)
    packed_a = pack_units(base, a_cyclic[0], a_mask[0], slots, n_layer, bs)
    packed_b = pack_b(b_mask, b_dense, b_cap, bs)
    size = (k_run, row_blocks, slots, bs)

    if not paired:
        units = lax.all_gather(packed_a, AXES, axis=0)
        units = units.reshape((-1,) + packed_a.shape[1:])
        per_run = n_col * n_layer * PARTS
        k_base = jnp.reshape(row, (1,)).astype(jnp.int32)
        partial = jnp.concatenate(
            [
                multiply_run([(units, r * per_run + u) for u in range(per_run)], packed_b, *size, k_base=k_base)
                for r in range(n_row)
            ],
            axis=0,
        )
        return lax.psum_scatter(partial, "row", scatter_dimension=0, tiled=True)

    def send(x, target):
        pairs = []
        for r in range(n_row):
            for h in range(2):
                for w in range(wide):
                    for l in range(n_layer):
                        to = target(r, h, w, l)
                        if to is None:
                            continue
                        tr, th, tw, tl = to
                        pairs.append((
                            (r * n_col + h * wide + w) * n_layer + l,
                            (tr * n_col + th * wide + tw) * n_layer + tl,
                        ))
        return lax.ppermute(x, AXES, pairs)

    power = n_layer & (n_layer - 1) == 0

    def along(m):
        if power:
            return lambda r, h, w, l: (r, h, w, l ^ m)
        return lambda r, h, w, l: (r, h, w, (l + m) % n_layer)

    def collect(mine):
        if n_layer == 4:
            over2 = send(mine, along(2))
            line = [mine, send(mine, along(1)), over2, send(over2, along(1))]
        else:
            line = [mine] + [send(mine, along(m)) for m in range(1, n_layer)]
        plane = line + [send(x, lambda r, h, w, l: (r, 1 - h, w, l)) for x in line]
        twin = [send(x, lambda r, h, w, l: (r, h, (w + d) % wide, l)) for d in range(1, wide) for x in plane]
        return [(x, at) for x in plane + twin for at in range(x.shape[0])]

    home = (col // wide) == row
    far = send(packed_a[1:], lambda r, h, w, l: None if r == h else (h, 1 - h, w, l))
    near = send(packed_a[:1], lambda r, h, w, l: (h, 1 - h if r == h else h, w, l))
    near, far, packed_b = lax.optimization_barrier((near, far, packed_b))
    theirs = collect(jnp.where(home, near, far))
    ours = collect(jnp.where(home, packed_a[1:], near))
    cut = j_run * 3 // 8
    parts = []
    for columns in ((0, cut), (cut, j_run)):
        part = multiply_run(theirs, packed_b, *size, columns=columns)
        parts.append(send(part, lambda r, h, w, l: (1 - r, h, w, l)))
    ours = multiply_run(ours, packed_b, *size)
    return ours + jnp.concatenate(parts, axis=1)


def solution(mesh):
    placed = (
        P("layer", "row", "col"),
        P("layer", "row", "col"),
        P("row", ("col", "layer")),
        P("row", ("col", "layer")),
    )
    return jax.shard_map(
        on_device, mesh=mesh, in_specs=placed, out_specs=P("row", ("col", "layer")), check_vma=False
    )
```

time: 720 us -> 152 us (0.21)
  waiting for transfers between devices: 306 us -> 61.1 us
  matrix products: 237 us -> 0 us
  local copies, waits for them, and re-layouts: 139 us -> 3.82 us
  Pallas kernels: 0 us -> 54 us
  starting transfers between devices: 0.04 us -> 27.4 us
  blocking collectives: 17.4 us -> 0 us
  between operations: 14.7 us -> 0.2 us
    all_gather x2 -> x0, waiting for transfers between devices: 306 us -> none  [the longest x1 280 us: on_device(): lax.all_gather(b_slots, 'row', axis=0, tiled=True)]
    dot_general x6 -> x0, matrix products: 237 us -> none  [the longest x2 106 us: accumulate(): jnp.einsum('smxa,sab->smxb', a_pieces, b_pieces, precision=precise)]
    gather x6 -> x0, local copies, waits for them, and re-layouts: 63 us -> none  [the longest x2 52.8 us: accumulate(): a_pieces = padded[where_rows]]
    ppermute x0 -> x34, waiting for transfers between devices: none -> 61.1 us  [send(): return lax.ppermute(x, AXES, pairs)]
    pallas_call x0 -> x5, Pallas kernels: none -> 54 us  [the longest x3 40.8 us: multiply_run(): pl.pallas_call(body, out_shape=jax.ShapeDtypeStruct((height, j_run * bs),...]
    unnamed x12 -> x17, local copies, waits for them, and re-layouts: 34.1 us -> 2.64 us
    ppermute x0 -> x34, starting transfers between devices: none -> 27.4 us  [send(): return lax.ppermute(x, AXES, pairs)]
    dynamic_slice x4 -> x0, local copies, waits for them, and re-layouts: 22.6 us -> none  [fold_piece(): lax.scan(add_source, running, (slot_groups, id_groups, source_rows))]
  transfers between devices with their start and end apart: 2 -> 34, of which waited for: 2 -> 13; matrix products, arithmetic and copies ran while one was open for 10% -> 0% of each run, Pallas kernels for 0% -> 34%
where the time goes in v1:
time: 152 us; the launch traced here: 149 us
  waiting for transfers between devices  61.1 us (40%)
  Pallas kernels  54 us (36%)
  starting transfers between devices  27.4 us (18%)
  local copies, waits for them, and re-layouts  3.82 us (3%)
  other arithmetic  2.31 us (2%)
    ppermute x34, waiting for transfers between devices, send(): return lax.ppermute(x, AXES, pairs)  61.1 us
    pallas_call x3, Pallas kernels, multiply_run(): pl.pallas_call(body, out_shape=jax.ShapeDtypeStruct((height, j_run * bs),...  40.8 us
    ppermute x34, starting transfers between devices, send(): return lax.ppermute(x, AXES, pairs)  27.4 us
    pallas_call x1, Pallas kernels, pack_b(): pl.pallas_call(body, out_shape=(jax.ShapeDtypeStruct((slots + 1, bs, 2 *...  10.4 us
  transfers between devices with their start and end apart: 34, of which 13 were waited for; matrix products, arithmetic and copies ran while one was open for 0% of the time, Pallas kernels for 34%

profile of v1, /device:TPU:0, one launch (start us, length us, event | category | flops | bytes accessed | tf_op | source)
XLA Modules:
  0.0 148.9 jit_solution(12788553300928191723)
XLA Ops:
  0.0 0.6 pad_add_fusion.base_ref
  0.7 2.9 %pack_units.1 = f32[2,776,128]{2,1,0:T(8,128)} custom-call(s32[2]{0:T(128)} %pad_add_fusion.base_ref, s32[4,8]{1,0:T(4,128)} %bitcast.5, f32[512,1024]{1,0:T(8,128)} %bitcast.4), custom_call_target="tpu_custom_call" | custom-call | tf_op jit(solution)/shard_map/pack_units/pallas_call | solution.py:68
  3.5 1.2 fusion
  4.7 0.7 collective-permute-start.1
  5.4 5.8 %collective-permute-start = (f32[1,776,128]{2,1,0:T(8,128)S(1)}, f32[1,776,128]{2,1,0:T(8,128)S(1)}, u32[]{:S(2)}, u32[]{:S(2)}) collective-permute-start(f32[1,776,128]{2,1,0:T(8,128)S(1)} %get-tuple-element.26), channel_id=1, source_target_pairs={{0,8},{1,9},{2,10},{3,11},{4,12},{5,13},{6,14},{7,15},{8,24},{9,25... | collective-permute-start | bytes 1191944 | tf_op jit(solution)/shard_map/ppermute | solution.py:348
  11.1 0.7 copy.5.bm_ref
  11.8 10.4 %pack_b.1 = (bf16[257,128,256]{2,1,0:T(8,128)(2,1)}, s32[256]{0:T(256)}, s32[9]{0:T(128)}, s32[8]{0:T(128)}) custom-call(s32[64,8]{1,0:T(8,128)} %copy.5.bm_ref, f32[8192,1024]{1,0:T(8,128)} %b_ref.1), custom_call_target="tpu_custom_call" | custom-call | tf_op jit(solution)/shard_map/pack_b/pallas_call | solution.py:139
  22.2 6.2 %collective-permute-done = f32[1,776,128]{2,1,0:T(8,128)S(1)} collective-permute-done((f32[1,776,128]{2,1,0:T(8,128)S(1)}, f32[1,776,128]{2,1,0:T(8,128)S(1)}, u32[]{:S(2)}, u32[]{:S(2)}) %collective-permute-start) | collective-permute-done | bytes 397344 | tf_op jit(solution)/shard_map/ppermute | solution.py:348
  28.4 0.1 broadcast_select_fusion
  28.5 2.8 %collective-permute-start.18 = (f32[1,776,128]{2,1,0:T(8,128)S(1)}, f32[1,776,128]{2,1,0:T(8,128)S(1)}, u32[]{:S(2)}, u32[]{:S(2)}) collective-permute-start(f32[1,776,128]{2,1,0:T(8,128)S(1)} %get-tuple-element.27.rest_0_), channel_id=1, source_target_pairs={{0,2},{1,3},{2,0},{3,1},{4,6},{5,7},{6,4},{7,5},{8,10},{9,11},{10,... | collective-permute-start | bytes 1191944 | tf_op jit(solution)/shard_map/ppermute | solution.py:348
  31.3 1.4 collective-permute-start.20
  32.7 0.6 collective-permute-start.5
  33.3 1.5 %collective-permute-start.17 = (f32[1,776,128]{2,1,0:T(8,128)S(1)}, f32[1,776,128]{2,1,0:T(8,128)S(1)}, u32[]{:S(2)}, u32[]{:S(2)}) collective-permute-start(f32[1,776,128]{2,1,0:T(8,128)S(1)} %get-tuple-element.27.rest_0_), channel_id=1, source_target_pairs={{0,1},{1,0},{2,3},{3,2},{4,5},{5,4},{6,7},{7,6},{8,9},{9,8},{10,11... | collective-permute-start | bytes 1191944 | tf_op jit(solution)/shard_map/ppermute | solution.py:348
  34.8 13.4 %collective-permute-done.18.rest_2_ = f32[1,776,128]{2,1,0:T(8,128)S(1)} collective-permute-done((f32[1,776,128]{2,1,0:T(8,128)S(1)}, f32[1,776,128]{2,1,0:T(8,128)S(1)}, u32[]{:S(2)}, u32[]{:S(2)}) %collective-permute-start.18) | collective-permute-done | bytes 397344 | tf_op jit(solution)/shard_map/ppermute | solution.py:348
  48.2 0.7 collective-permute-start.19
  48.9 1.4 collective-permute-done.5.rest_4_
  50.3 1.7 %collective-permute-start.22 = (f32[1,776,128]{2,1,0:T(8,128)S(1)}, f32[1,776,128]{2,1,0:T(8,128)S(1)}, u32[]{:S(2)}, u32[]{:S(2)}) collective-permute-start(f32[1,776,128]{2,1,0:T(8,128)S(1)} %collective-permute-done.18.rest_2_), channel_id=1, source_target_pairs={{0,8},{1,9},{2,10},{3,11},{4,12},{5,13},{6,14},{7,15},{8,0},{9,1},... | collective-permute-start | bytes 1191944 | tf_op jit(solution)/shard_map/ppermute | solution.py:348
  52.1 0.7 collective-permute-done.17.rest_1_
  52.8 1.4 collective-permute-start.21
  54.2 6.7 %collective-permute-done.19.rest_3_ = f32[1,776,128]{2,1,0:T(8,128)S(1)} collective-permute-done((f32[1,776,128]{2,1,0:T(8,128)S(1)}, f32[1,776,128]{2,1,0:T(8,128)S(1)}, u32[]{:S(2)}, u32[]{:S(2)}) %collective-permute-start.19) | collective-permute-done | bytes 397344 | tf_op jit(solution)/shard_map/ppermute | solution.py:348
  60.9 1.4 collective-permute-start.23
  62.3 0.1 collective-permute-done.22.rest_6_
  62.4 0.4 collective-permute-start.30
  62.8 0.1 collective-permute-start.27
  62.9 8.0 %collective-permute-done.21.rest_5_ = f32[1,776,128]{2,1,0:T(8,128)S(1)} collective-permute-done((f32[1,776,128]{2,1,0:T(8,128)S(1)}, f32[1,776,128]{2,1,0:T(8,128)S(1)}, u32[]{:S(2)}, u32[]{:S(2)}) %collective-permute-start.21) | collective-permute-done | bytes 397344 | tf_op jit(solution)/shard_map/ppermute | solution.py:348
  70.9 7.4 %collective-permute-done.23.rest_7_ = f32[1,776,128]{2,1,0:T(8,128)S(1)} collective-permute-done((f32[1,776,128]{2,1,0:T(8,128)S(1)}, f32[1,776,128]{2,1,0:T(8,128)S(1)}, u32[]{:S(2)}, u32[]{:S(2)}) %collective-permute-start.23) | collective-permute-done | bytes 397344 | tf_op jit(solution)/shard_map/ppermute | solution.py:348
  78.3 3.4 %collective-permute-start.3 = (f32[1,776,128]{2,1,0:T(8,128)S(1)}, f32[1,776,128]{2,1,0:T(8,128)S(1)}, u32[]{:S(2)}, u32[]{:S(2)}) collective-permute-start(f32[1,776,128]{2,1,0:T(8,128)S(1)} %get-tuple-element.28.rest_0_), channel_id=1, source_target_pairs={{0,2},{1,3},{2,0},{3,1},{4,6},{5,7},{6,4},{7,5},{8,10},{9,11},{10,... | collective-permute-start | bytes 1191944 | tf_op jit(solution)/shard_map/ppermute | solution.py:348
  81.7 0.2 collective-permute-start.9
  82.0 0.3 collective-permute-start.13
  82.3 0.7 copy-done
  83.0 0.7 copy-done.2
  83.6 0.6 copy-done.4
  84.3 13.2 %multiply_run.5 = f32[512,640]{1,0:T(8,128)S(1)} custom-call(s32[256]{0:T(256)S(1)} %copy-done, s32[9]{0:T(128)S(1)} %copy-done.2, s32[8]{0:T(128)S(1)} %copy-done.4, s32[1]{0:T(128)} %constant.35.clone.1.base_ref, bf16[257,128,256]{2,1,0:T(8,128)(2,1)} %get-tuple-element.22.bw_ref, f32[1,776,128]{2,1,0:T(8,128)S(1)} %get-tuple-element.27.rest_0_, ...), custom_call_target="tpu_custom_call" | custom-call | tf_op jit(solution)/shard_map/multiply_run/pallas_call | solution.py:280
  97.5 0.1 collective-permute-start.33
  97.6 2.7 %collective-permute-done.3.rest_2_ = f32[1,776,128]{2,1,0:T(8,128)S(1)} collective-permute-done((f32[1,776,128]{2,1,0:T(8,128)S(1)}, f32[1,776,128]{2,1,0:T(8,128)S(1)}, u32[]{:S(2)}, u32[]{:S(2)}) %collective-permute-start.3) | collective-permute-done | bytes 397344 | tf_op jit(solution)/shard_map/ppermute | solution.py:348
  100.2 1.7 %collective-permute-start.7 = (f32[1,776,128]{2,1,0:T(8,128)S(1)}, f32[1,776,128]{2,1,0:T(8,128)S(1)}, u32[]{:S(2)}, u32[]{:S(2)}) collective-permute-start(f32[1,776,128]{2,1,0:T(8,128)S(1)} %collective-permute-done.3.rest_2_), channel_id=1, source_target_pairs={{0,8},{1,9},{2,10},{3,11},{4,12},{5,13},{6,14},{7,15},{8,0},{9,1},... | collective-permute-start | bytes 1191944 | tf_op jit(solution)/shard_map/ppermute | solution.py:348
  102.0 0.3 collective-permute-start.10
  102.3 1.4 collective-permute-start.6
  103.7 8.6 %collective-permute-done.7.rest_6_ = f32[1,776,128]{2,1,0:T(8,128)S(1)} collective-permute-done((f32[1,776,128]{2,1,0:T(8,128)S(1)}, f32[1,776,128]{2,1,0:T(8,128)S(1)}, u32[]{:S(2)}, u32[]{:S(2)}) %collective-permute-start.7) | collective-permute-done | bytes 397344 | tf_op jit(solution)/shard_map/ppermute | solution.py:348
  112.3 1.0 collective-permute-done.4.rest_3_
  113.3 0.7 collective-permute-start.8
  114.1 10.9 %multiply_run.4 = f32[512,384]{1,0:T(8,128)S(1)} custom-call(s32[256]{0:T(256)S(1)} %copy-done, s32[9]{0:T(128)S(1)} %copy-done.2, s32[8]{0:T(128)S(1)} %copy-done.4, s32[1]{0:T(128)} %constant.35.clone.1.base_ref, bf16[257,128,256]{2,1,0:T(8,128)(2,1)} %get-tuple-element.22.bw_ref, f32[1,776,128]{2,1,0:T(8,128)S(1)} %get-tuple-element.27.rest_0_, ...), custom_call_target="tpu_custom_call" | custom-call | tf_op jit(solution)/shard_map/multiply_run/pallas_call | solution.py:280
  125.1 0.1 collective-permute-start.12
  125.2 0.5 collective-permute-start.14
  125.7 3.2 %collective-permute-done.8.rest_7_ = f32[1,776,128]{2,1,0:T(8,128)S(1)} collective-permute-done((f32[1,776,128]{2,1,0:T(8,128)S(1)}, f32[1,776,128]{2,1,0:T(8,128)S(1)}, u32[]{:S(2)}, u32[]{:S(2)}) %collective-permute-start.8) | collective-permute-done | bytes 397344 | tf_op jit(solution)/shard_map/ppermute | solution.py:348
  128.9 1.7 %collective-permute-done.16.rest_15_ = f32[1,776,128]{2,1,0:T(8,128)S(1)} collective-permute-done((f32[1,776,128]{2,1,0:T(8,128)S(1)}, f32[1,776,128]{2,1,0:T(8,128)S(1)}, u32[]{:S(2)}, u32[]{:S(2)}) %collective-permute-start.16) | collective-permute-done | bytes 397344 | tf_op jit(solution)/shard_map/ppermute | solution.py:348
  130.6 16.7 %multiply_run.3 = f32[512,1024]{1,0:T(8,128)S(1)} custom-call(s32[256]{0:T(256)S(1)} %copy-done.1, s32[9]{0:T(128)S(1)} %copy-done.3, s32[8]{0:T(128)S(1)} %copy-done.5, s32[1]{0:T(128)} %constant.35.clone.1.base_ref, bf16[257,128,256]{2,1,0:T(8,128)(2,1)} %get-tuple-element.22.bw_ref, f32[1,776,128]{2,1,0:T(8,128)S(1)} %get-tuple-element.28.rest_0_, ...), custom_call_target="tpu_custom_call" | custom-call | tf_op jit(solution)/shard_map/multiply_run/pallas_call | solution.py:280
  147.3 1.6 %maximum_add_fusion = f32[512,1024]{1,0:T(8,128)} fusion(f32[512,1024]{1,0:T(8,128)S(1)} %multiply_run.3, f32[512,640]{1,0:T(8,128)S(1)} %collective-permute-done.33, f32[512,384]{1,0:T(8,128)S(1)} %collective-permute-done.32), kind=kLoop, calls=%fused_computation | loop fusion | flops 1048576 | bytes 6291456 | tf_op jit(solution)/shard_map/add | solution.py:379
  (46 shorter events, 0.2 us)
Async XLA Ops:
  0.6 10.5 %copy-start.7 = (s32[64,8]{0,1:T(8,128)S(1)}, s32[64,8]{0,1:T(8,128)}, u32[]{:S(2)}) copy-start(s32[64,8]{0,1:T(8,128)} %param.7) | copy-start | bytes 6148
  4.7 17.5 %collective-permute-start.1 = (f32[1,776,128]{2,1,0:T(8,128)S(1)}, f32[1,776,128]{2,1,0:T(8,128)S(1)}, u32[]{:S(2)}, u32[]{:S(2)}) collective-permute-start(f32[1,776,128]{2,1,0:T(8,128)S(1)} %get-tuple-element.25), channel_id=1, source_target_pairs={{8,16},{9,17},{10,18},{11,19},{12,20},{13,21},{14,22},{15,23},{16,... | collective-permute-start | bytes 1191944 | tf_op jit(solution)/shard_map/ppermute | solution.py:348
  5.4 23.1 %collective-permute-start = (f32[1,776,128]{2,1,0:T(8,128)S(1)}, f32[1,776,128]{2,1,0:T(8,128)S(1)}, u32[]{:S(2)}, u32[]{:S(2)}) collective-permute-start(f32[1,776,128]{2,1,0:T(8,128)S(1)} %get-tuple-element.26), channel_id=1, source_target_pairs={{0,8},{1,9},{2,10},{3,11},{4,12},{5,13},{6,14},{7,15},{8,24},{9,25... | collective-permute-start | bytes 1191944 | tf_op jit(solution)/shard_map/ppermute | solution.py:348
  11.8 16.6 %copy-start.6 = (f32[2,776,128]{2,1,0:T(8,128)S(1)}, f32[2,776,128]{2,1,0:T(8,128)}, u32[]{:S(2)}) copy-start(f32[2,776,128]{2,1,0:T(8,128)} %pack_units.1) | copy-start | bytes 2383876
  28.5 19.7 %collective-permute-start.18 = (f32[1,776,128]{2,1,0:T(8,128)S(1)}, f32[1,776,128]{2,1,0:T(8,128)S(1)}, u32[]{:S(2)}, u32[]{:S(2)}) collective-permute-start(f32[1,776,128]{2,1,0:T(8,128)S(1)} %get-tuple-element.27.rest_0_), channel_id=1, source_target_pairs={{0,2},{1,3},{2,0},{3,1},{4,6},{5,7},{6,4},{7,5},{8,10},{9,11},{10,... | collective-permute-start | bytes 1191944 | tf_op jit(solution)/shard_map/ppermute | solution.py:348
  31.3 17.6 %collective-permute-start.20 = (f32[1,776,128]{2,1,0:T(8,128)S(1)}, f32[1,776,128]{2,1,0:T(8,128)S(1)}, u32[]{:S(2)}, u32[]{:S(2)}) collective-permute-start(f32[1,776,128]{2,1,0:T(8,128)S(1)} %get-tuple-element.27.rest_0_), channel_id=1, source_target_pairs={{0,8},{1,9},{2,10},{3,11},{4,12},{5,13},{6,14},{7,15},{8,0},{9,1},... | collective-permute-start | bytes 1191944 | tf_op jit(solution)/shard_map/ppermute | solution.py:348
  32.7 17.6 %collective-permute-start.5 = (f32[1,776,128]{2,1,0:T(8,128)S(1)}, f32[1,776,128]{2,1,0:T(8,128)S(1)}, u32[]{:S(2)}, u32[]{:S(2)}) collective-permute-start(f32[1,776,128]{2,1,0:T(8,128)S(1)} %get-tuple-element.28.rest_0_), channel_id=1, source_target_pairs={{0,8},{1,9},{2,10},{3,11},{4,12},{5,13},{6,14},{7,15},{8,0},{9,1},... | collective-permute-start | bytes 1191944 | tf_op jit(solution)/shard_map/ppermute | solution.py:348
  33.3 18.8 %collective-permute-start.24 = (f32[1,776,128]{2,1,0:T(8,128)S(1)}, f32[1,776,128]{2,1,0:T(8,128)S(1)}, u32[]{:S(2)}, u32[]{:S(2)}) collective-permute-start(f32[1,776,128]{2,1,0:T(8,128)S(1)} %get-tuple-element.27.rest_0_), channel_id=1, source_target_pairs={{0,4},{1,5},{2,6},{3,7},{4,0},{5,1},{6,2},{7,3},{8,12},{9,13},{10,... | collective-permute-start | bytes 1191944 | tf_op jit(solution)/shard_map/ppermute | solution.py:348
  33.3 19.5 %collective-permute-start.17 = (f32[1,776,128]{2,1,0:T(8,128)S(1)}, f32[1,776,128]{2,1,0:T(8,128)S(1)}, u32[]{:S(2)}, u32[]{:S(2)}) collective-permute-start(f32[1,776,128]{2,1,0:T(8,128)S(1)} %get-tuple-element.27.rest_0_), channel_id=1, source_target_pairs={{0,1},{1,0},{2,3},{3,2},{4,5},{5,4},{6,7},{7,6},{8,9},{9,8},{10,11... | collective-permute-start | bytes 1191944 | tf_op jit(solution)/shard_map/ppermute | solution.py:348
  48.2 12.6 %collective-permute-start.19 = (f32[1,776,128]{2,1,0:T(8,128)S(1)}, f32[1,776,128]{2,1,0:T(8,128)S(1)}, u32[]{:S(2)}, u32[]{:S(2)}) collective-permute-start(f32[1,776,128]{2,1,0:T(8,128)S(1)} %collective-permute-done.18.rest_2_), channel_id=1, source_target_pairs={{0,1},{1,0},{2,3},{3,2},{4,5},{5,4},{6,7},{7,6},{8,9},{9,8},{10,11... | collective-permute-start | bytes 1191944 | tf_op jit(solution)/shard_map/ppermute | solution.py:348
  48.9 13.3 %collective-permute-start.28 = (f32[1,776,128]{2,1,0:T(8,128)S(1)}, f32[1,776,128]{2,1,0:T(8,128)S(1)}, u32[]{:S(2)}, u32[]{:S(2)}) collective-permute-start(f32[1,776,128]{2,1,0:T(8,128)S(1)} %collective-permute-done.20.rest_4_), channel_id=1, source_target_pairs={{0,4},{1,5},{2,6},{3,7},{4,0},{5,1},{6,2},{7,3},{8,12},{9,13},{10,... | collective-permute-start | bytes 1191944 | tf_op jit(solution)/shard_map/ppermute | solution.py:348
  50.3 12.1 %collective-permute-start.22 = (f32[1,776,128]{2,1,0:T(8,128)S(1)}, f32[1,776,128]{2,1,0:T(8,128)S(1)}, u32[]{:S(2)}, u32[]{:S(2)}) collective-permute-start(f32[1,776,128]{2,1,0:T(8,128)S(1)} %collective-permute-done.18.rest_2_), channel_id=1, source_target_pairs={{0,8},{1,9},{2,10},{3,11},{4,12},{5,13},{6,14},{7,15},{8,0},{9,1},... | collective-permute-start | bytes 1191944 | tf_op jit(solution)/shard_map/ppermute | solution.py:348
  52.1 10.7 %collective-permute-start.26 = (f32[1,776,128]{2,1,0:T(8,128)S(1)}, f32[1,776,128]{2,1,0:T(8,128)S(1)}, u32[]{:S(2)}, u32[]{:S(2)}) collective-permute-start(f32[1,776,128]{2,1,0:T(8,128)S(1)} %collective-permute-done.18.rest_2_), channel_id=1, source_target_pairs={{0,4},{1,5},{2,6},{3,7},{4,0},{5,1},{6,2},{7,3},{8,12},{9,13},{10,... | collective-permute-start | bytes 1191944 | tf_op jit(solution)/shard_map/ppermute | solution.py:348
  52.8 18.1 %collective-permute-start.21 = (f32[1,776,128]{2,1,0:T(8,128)S(1)}, f32[1,776,128]{2,1,0:T(8,128)S(1)}, u32[]{:S(2)}, u32[]{:S(2)}) collective-permute-start(f32[1,776,128]{2,1,0:T(8,128)S(1)} %collective-permute-done.17.rest_1_), channel_id=1, source_target_pairs={{0,8},{1,9},{2,10},{3,11},{4,12},{5,13},{6,14},{7,15},{8,0},{9,1},... | collective-permute-start | bytes 1191944 | tf_op jit(solution)/shard_map/ppermute | solution.py:348
  60.9 17.4 %collective-permute-start.23 = (f32[1,776,128]{2,1,0:T(8,128)S(1)}, f32[1,776,128]{2,1,0:T(8,128)S(1)}, u32[]{:S(2)}, u32[]{:S(2)}) collective-permute-start(f32[1,776,128]{2,1,0:T(8,128)S(1)} %collective-permute-done.19.rest_3_), channel_id=1, source_target_pairs={{0,8},{1,9},{2,10},{3,11},{4,12},{5,13},{6,14},{7,15},{8,0},{9,1},... | collective-permute-start | bytes 1191944 | tf_op jit(solution)/shard_map/ppermute | solution.py:348
  62.3 16.0 %collective-permute-start.25 = (f32[1,776,128]{2,1,0:T(8,128)S(1)}, f32[1,776,128]{2,1,0:T(8,128)S(1)}, u32[]{:S(2)}, u32[]{:S(2)}) collective-permute-start(f32[1,776,128]{2,1,0:T(8,128)S(1)} %collective-permute-done.17.rest_1_), channel_id=1, source_target_pairs={{0,4},{1,5},{2,6},{3,7},{4,0},{5,1},{6,2},{7,3},{8,12},{9,13},{10,... | collective-permute-start | bytes 1191944 | tf_op jit(solution)/shard_map/ppermute | solution.py:348
  62.4 19.3 %collective-permute-start.30 = (f32[1,776,128]{2,1,0:T(8,128)S(1)}, f32[1,776,128]{2,1,0:T(8,128)S(1)}, u32[]{:S(2)}, u32[]{:S(2)}) collective-permute-start(f32[1,776,128]{2,1,0:T(8,128)S(1)} %collective-permute-done.22.rest_6_), channel_id=1, source_target_pairs={{0,4},{1,5},{2,6},{3,7},{4,0},{5,1},{6,2},{7,3},{8,12},{9,13},{10,... | collective-permute-start | bytes 1191944 | tf_op jit(solution)/shard_map/ppermute | solution.py:348
  62.8 19.2 %collective-permute-start.27 = (f32[1,776,128]{2,1,0:T(8,128)S(1)}, f32[1,776,128]{2,1,0:T(8,128)S(1)}, u32[]{:S(2)}, u32[]{:S(2)}) collective-permute-start(f32[1,776,128]{2,1,0:T(8,128)S(1)} %collective-permute-done.19.rest_3_), channel_id=1, source_target_pairs={{0,4},{1,5},{2,6},{3,7},{4,0},{5,1},{6,2},{7,3},{8,12},{9,13},{10,... | collective-permute-start | bytes 1191944 | tf_op jit(solution)/shard_map/ppermute | solution.py:348
  70.9 11.1 %collective-permute-start.29 = (f32[1,776,128]{2,1,0:T(8,128)S(1)}, f32[1,776,128]{2,1,0:T(8,128)S(1)}, u32[]{:S(2)}, u32[]{:S(2)}) collective-permute-start(f32[1,776,128]{2,1,0:T(8,128)S(1)} %collective-permute-done.21.rest_5_), channel_id=1, source_target_pairs={{0,4},{1,5},{2,6},{3,7},{4,0},{5,1},{6,2},{7,3},{8,12},{9,13},{10,... | collective-permute-start | bytes 1191944 | tf_op jit(solution)/shard_map/ppermute | solution.py:348
  78.3 4.0 %collective-permute-start.31 = (f32[1,776,128]{2,1,0:T(8,128)S(1)}, f32[1,776,128]{2,1,0:T(8,128)S(1)}, u32[]{:S(2)}, u32[]{:S(2)}) collective-permute-start(f32[1,776,128]{2,1,0:T(8,128)S(1)} %collective-permute-done.23.rest_7_), channel_id=1, source_target_pairs={{0,4},{1,5},{2,6},{3,7},{4,0},{5,1},{6,2},{7,3},{8,12},{9,13},{10,... | collective-permute-start | bytes 1191944 | tf_op jit(solution)/shard_map/ppermute | solution.py:348
  78.3 21.9 %collective-permute-start.3 = (f32[1,776,128]{2,1,0:T(8,128)S(1)}, f32[1,776,128]{2,1,0:T(8,128)S(1)}, u32[]{:S(2)}, u32[]{:S(2)}) collective-permute-start(f32[1,776,128]{2,1,0:T(8,128)S(1)} %get-tuple-element.28.rest_0_), channel_id=1, source_target_pairs={{0,2},{1,3},{2,0},{3,1},{4,6},{5,7},{6,4},{7,5},{8,10},{9,11},{10,... | collective-permute-start | bytes 1191944 | tf_op jit(solution)/shard_map/ppermute | solution.py:348
  81.7 18.5 %collective-permute-start.9 = (f32[1,776,128]{2,1,0:T(8,128)S(1)}, f32[1,776,128]{2,1,0:T(8,128)S(1)}, u32[]{:S(2)}, u32[]{:S(2)}) collective-permute-start(f32[1,776,128]{2,1,0:T(8,128)S(1)} %get-tuple-element.28.rest_0_), channel_id=1, source_target_pairs={{0,4},{1,5},{2,6},{3,7},{4,0},{5,1},{6,2},{7,3},{8,12},{9,13},{10,... | collective-permute-start | bytes 1191944 | tf_op jit(solution)/shard_map/ppermute | solution.py:348
  82.0 20.0 %collective-permute-start.2 = (f32[1,776,128]{2,1,0:T(8,128)S(1)}, f32[1,776,128]{2,1,0:T(8,128)S(1)}, u32[]{:S(2)}, u32[]{:S(2)}) collective-permute-start(f32[1,776,128]{2,1,0:T(8,128)S(1)} %get-tuple-element.28.rest_0_), channel_id=1, source_target_pairs={{0,1},{1,0},{2,3},{3,2},{4,5},{5,4},{6,7},{7,6},{8,9},{9,8},{10,11... | collective-permute-start | bytes 1191944 | tf_op jit(solution)/shard_map/ppermute | solution.py:348
  82.0 20.0 %collective-permute-start.13 = (f32[1,776,128]{2,1,0:T(8,128)S(1)}, f32[1,776,128]{2,1,0:T(8,128)S(1)}, u32[]{:S(2)}, u32[]{:S(2)}) collective-permute-start(f32[1,776,128]{2,1,0:T(8,128)S(1)} %collective-permute-done.5.rest_4_), channel_id=1, source_target_pairs={{0,4},{1,5},{2,6},{3,7},{4,0},{5,1},{6,2},{7,3},{8,12},{9,13},{10,... | collective-permute-start | bytes 1191944 | tf_op jit(solution)/shard_map/ppermute | solution.py:348
  82.3 0.7 copy-start
  83.0 0.7 copy-start.2
  83.6 0.6 copy-start.4
  97.5 33.1 %copy-start.1 = (s32[256]{0:T(256)S(1)}, s32[256]{0:T(256)}, u32[]{:S(2)}) copy-start(s32[256]{0:T(256)} %get-tuple-element.19.bk_ref) | copy-start | bytes 3076
  97.5 33.1 %copy-start.3 = (s32[9]{0:T(128)S(1)}, s32[9]{0:T(128)}, u32[]{:S(2)}) copy-start(s32[9]{0:T(128)} %get-tuple-element.20.bs_ref) | copy-start | bytes 112
  97.5 33.1 %copy-start.5 = (s32[8]{0:T(128)S(1)}, s32[8]{0:T(128)}, u32[]{:S(2)}) copy-start(s32[8]{0:T(128)} %get-tuple-element.21.be_ref) | copy-start | bytes 100
  97.5 49.8 %collective-permute-start.33 = (f32[512,640]{1,0:T(8,128)S(1)}, f32[512,640]{1,0:T(8,128)S(1)}, u32[]{:S(2)}, u32[]{:S(2)}) collective-permute-start(f32[512,640]{1,0:T(8,128)S(1)} %multiply_run.5), channel_id=1, source_target_pairs={{0,16},{1,17},{2,18},{3,19},{4,20},{5,21},{6,22},{7,23},{8,24},{9,... | collective-permute-start | bytes 3932168 | tf_op jit(solution)/shard_map/ppermute | solution.py:348
  100.2 2.1 %collective-permute-start.11 = (f32[1,776,128]{2,1,0:T(8,128)S(1)}, f32[1,776,128]{2,1,0:T(8,128)S(1)}, u32[]{:S(2)}, u32[]{:S(2)}) collective-permute-start(f32[1,776,128]{2,1,0:T(8,128)S(1)} %collective-permute-done.3.rest_2_), channel_id=1, source_target_pairs={{0,4},{1,5},{2,6},{3,7},{4,0},{5,1},{6,2},{7,3},{8,12},{9,13},{10,... | collective-permute-start | bytes 1191944 | tf_op jit(solution)/shard_map/ppermute | solution.py:348
  100.2 12.1 %collective-permute-start.7 = (f32[1,776,128]{2,1,0:T(8,128)S(1)}, f32[1,776,128]{2,1,0:T(8,128)S(1)}, u32[]{:S(2)}, u32[]{:S(2)}) collective-permute-start(f32[1,776,128]{2,1,0:T(8,128)S(1)} %collective-permute-done.3.rest_2_), channel_id=1, source_target_pairs={{0,8},{1,9},{2,10},{3,11},{4,12},{5,13},{6,14},{7,15},{8,0},{9,1},... | collective-permute-start | bytes 1191944 | tf_op jit(solution)/shard_map/ppermute | solution.py:348
  102.0 11.3 %collective-permute-start.4 = (f32[1,776,128]{2,1,0:T(8,128)S(1)}, f32[1,776,128]{2,1,0:T(8,128)S(1)}, u32[]{:S(2)}, u32[]{:S(2)}) collective-permute-start(f32[1,776,128]{2,1,0:T(8,128)S(1)} %collective-permute-done.3.rest_2_), channel_id=1, source_target_pairs={{0,1},{1,0},{2,3},{3,2},{4,5},{5,4},{6,7},{7,6},{8,9},{9,8},{10,11... | collective-permute-start | bytes 1191944 | tf_op jit(solution)/shard_map/ppermute | solution.py:348
  102.0 23.0 %collective-permute-start.10 = (f32[1,776,128]{2,1,0:T(8,128)S(1)}, f32[1,776,128]{2,1,0:T(8,128)S(1)}, u32[]{:S(2)}, u32[]{:S(2)}) collective-permute-start(f32[1,776,128]{2,1,0:T(8,128)S(1)} %collective-permute-done.2.rest_1_), channel_id=1, source_target_pairs={{0,4},{1,5},{2,6},{3,7},{4,0},{5,1},{6,2},{7,3},{8,12},{9,13},{10,... | collective-permute-start | bytes 1191944 | tf_op jit(solution)/shard_map/ppermute | solution.py:348
  102.3 22.8 %collective-permute-start.6 = (f32[1,776,128]{2,1,0:T(8,128)S(1)}, f32[1,776,128]{2,1,0:T(8,128)S(1)}, u32[]{:S(2)}, u32[]{:S(2)}) collective-permute-start(f32[1,776,128]{2,1,0:T(8,128)S(1)} %collective-permute-done.2.rest_1_), channel_id=1, source_target_pairs={{0,8},{1,9},{2,10},{3,11},{4,12},{5,13},{6,14},{7,15},{8,0},{9,1},... | collective-permute-start | bytes 1191944 | tf_op jit(solution)/shard_map/ppermute | solution.py:348
  112.3 12.9 %collective-permute-start.15 = (f32[1,776,128]{2,1,0:T(8,128)S(1)}, f32[1,776,128]{2,1,0:T(8,128)S(1)}, u32[]{:S(2)}, u32[]{:S(2)}) collective-permute-start(f32[1,776,128]{2,1,0:T(8,128)S(1)} %collective-permute-done.7.rest_6_), channel_id=1, source_target_pairs={{0,4},{1,5},{2,6},{3,7},{4,0},{5,1},{6,2},{7,3},{8,12},{9,13},{10,... | collective-permute-start | bytes 1191944 | tf_op jit(solution)/shard_map/ppermute | solution.py:348
  113.3 15.6 %collective-permute-start.8 = (f32[1,776,128]{2,1,0:T(8,128)S(1)}, f32[1,776,128]{2,1,0:T(8,128)S(1)}, u32[]{:S(2)}, u32[]{:S(2)}) collective-permute-start(f32[1,776,128]{2,1,0:T(8,128)S(1)} %collective-permute-done.4.rest_3_), channel_id=1, source_target_pairs={{0,8},{1,9},{2,10},{3,11},{4,12},{5,13},{6,14},{7,15},{8,0},{9,1},... | collective-permute-start | bytes 1191944 | tf_op jit(solution)/shard_map/ppermute | solution.py:348
  125.0 22.3 %collective-permute-start.32 = (f32[512,384]{1,0:T(8,128)S(1)}, f32[512,384]{1,0:T(8,128)S(1)}, u32[]{:S(2)}, u32[]{:S(2)}) collective-permute-start(f32[512,384]{1,0:T(8,128)S(1)} %multiply_run.4), channel_id=1, source_target_pairs={{0,16},{1,17},{2,18},{3,19},{4,20},{5,21},{6,22},{7,23},{8,24},{9,... | collective-permute-start | bytes 2359304 | tf_op jit(solution)/shard_map/ppermute | solution.py:348
  125.1 3.8 %collective-permute-start.12 = (f32[1,776,128]{2,1,0:T(8,128)S(1)}, f32[1,776,128]{2,1,0:T(8,128)S(1)}, u32[]{:S(2)}, u32[]{:S(2)}) collective-permute-start(f32[1,776,128]{2,1,0:T(8,128)S(1)} %collective-permute-done.4.rest_3_), channel_id=1, source_target_pairs={{0,4},{1,5},{2,6},{3,7},{4,0},{5,1},{6,2},{7,3},{8,12},{9,13},{10,... | collective-permute-start | bytes 1191944 | tf_op jit(solution)/shard_map/ppermute | solution.py:348
  125.2 3.7 %collective-permute-start.14 = (f32[1,776,128]{2,1,0:T(8,128)S(1)}, f32[1,776,128]{2,1,0:T(8,128)S(1)}, u32[]{:S(2)}, u32[]{:S(2)}) collective-permute-start(f32[1,776,128]{2,1,0:T(8,128)S(1)} %collective-permute-done.6.rest_5_), channel_id=1, source_target_pairs={{0,4},{1,5},{2,6},{3,7},{4,0},{5,1},{6,2},{7,3},{8,12},{9,13},{10,... | collective-permute-start | bytes 1191944 | tf_op jit(solution)/shard_map/ppermute | solution.py:348
  128.9 1.7 %collective-permute-start.16 = (f32[1,776,128]{2,1,0:T(8,128)S(1)}, f32[1,776,128]{2,1,0:T(8,128)S(1)}, u32[]{:S(2)}, u32[]{:S(2)}) collective-permute-start(f32[1,776,128]{2,1,0:T(8,128)S(1)} %collective-permute-done.8.rest_7_), channel_id=1, source_target_pairs={{0,4},{1,5},{2,6},{3,7},{4,0},{5,1},{6,2},{7,3},{8,12},{9,13},{10,... | collective-permute-start | bytes 1191944 | tf_op jit(solution)/shard_map/ppermute | solution.py:348
